TPU v7x, 32 devices: a whole 2x2x4 slice. The times are simulated.
32 devices in a mesh: section: 4 (over z), tensor: 4 (over y, x), dp: 2 (over core).
Axes of the slice: x: 2, y: 2, z: 4, core: 2. Of those that a mesh axis runs over, the one named last changes fastest.
Arguments:
- enc_hidden: bfloat16 [128, 2048], P(('dp', 'tensor'), 'section'), parts along dimension 0, may hold values from -70 to 70
- mlp_gain: float32 [2048], P('section'), may hold values from 0.25 to 1.75
- final_gain: float32 [2048], P('section'), may hold values from 0.25 to 1.75
- w_gate: bfloat16 [2048, 8192], P('section', 'tensor'), may hold values from -0.125 to 0.125
- w_up: bfloat16 [2048, 8192], P('section', 'tensor'), may hold values from -0.125 to 0.125
- w_down: bfloat16 [8192, 2048], P('tensor', 'section'), may hold values from -0.0625 to 0.0625
- key_weight: bfloat16 [4, 2048, 4096], P('section', None, 'tensor'), may hold values from -0.125 to 0.125
- value_weight: bfloat16 [4, 2048, 4096], P('section', None, 'tensor'), may hold values from -0.125 to 0.125
- queries: bfloat16 [4, 2048, 4096], P('section', 'dp', 'tensor'), parts along dimension 1, may hold values from -340 to 340
- context_grad: bfloat16 [4, 2048, 4096], P('section', 'dp', 'tensor'), parts along dimension 1, may hold values from -6 to 6
Outputs:
- query_grad: bfloat16 [4, 2048, 4096], P('section', 'dp', 'tensor'), parts along dimension 1
- hidden_grad: float32 [128, 2048], P(('dp', 'tensor'), 'section'), parts along dimension 0
- gate_weight_grad: bfloat16 [4096, 8192], P(('dp', 'section'), 'tensor'), parts along dimension 0
- up_weight_grad: bfloat16 [4096, 8192], P(('dp', 'section'), 'tensor'), parts along dimension 0
- down_weight_grad: bfloat16 [16384, 2048], P(('dp', 'tensor'), 'section'), parts along dimension 0
There are 2 independent parts, one for each index of `dp`. A program takes and returns all parts, laid end to end along the dimension named above; an argument that names none is the same for every part. Nothing has to cross between parts.
All inputs are finite; a program needn't handle non-finite values.
Results may differ from a plain program's by a relative error of at most 0.017.
Values may be sent and summed in bfloat16 or wider, within the bound.
A program may use at most 64 MiB of HBM per device.

v0:
```python
import jax
import jax.numpy as jnp
from jax import lax
from jax.sharding import PartitionSpec as P

D = 2048
HEAD = 256


EPSILON = 1e-06


def attend(query_block, grad_block, keys, values):
    scale_factor = HEAD ** (-0.5)
    tgt_rows = query_block.shape[0]
    src_rows = keys.shape[0]
    heads_here = query_block.shape[1] // HEAD
    query_heads = query_block.reshape(tgt_rows, heads_here, HEAD)
    key_heads = keys.reshape(src_rows, heads_here, HEAD)
    value_heads = values.reshape(src_rows, heads_here, HEAD)
    grad_heads = grad_block.reshape(tgt_rows, heads_here, HEAD)
    scores = (
        jnp.einsum("qhd,khd->hqk", query_heads, key_heads, preferred_element_type=jnp.float32)
        * scale_factor
    )
    probs = jax.nn.softmax(scores, axis=-1)
    probs_bf = probs.astype(jnp.bfloat16)
    context = jnp.einsum("hqk,khd->qhd", probs_bf, value_heads, preferred_element_type=jnp.float32)
    delta = jnp.sum(grad_heads.astype(jnp.float32) * context, axis=2)
    dprob = jnp.einsum("qhd,khd->hqk", grad_heads, value_heads, preferred_element_type=jnp.float32)
    dscore = (probs * (dprob - jnp.transpose(delta)[:, :, None]) * scale_factor).astype(
        jnp.bfloat16
    )
    query_grad = jnp.einsum(
        "hqk,khd->qhd", dscore, key_heads, preferred_element_type=jnp.float32
    ).astype(jnp.bfloat16)
    key_grad = jnp.einsum(
        "hqk,qhd->khd", dscore, query_heads, preferred_element_type=jnp.float32
    ).astype(jnp.bfloat16)
    value_grad = jnp.einsum(
        "hqk,qhd->khd", probs_bf, grad_heads, preferred_element_type=jnp.float32
    ).astype(jnp.bfloat16)
    width = heads_here * HEAD
    return (
        query_grad.reshape(tgt_rows, width),
        key_grad.reshape(src_rows, width),
        value_grad.reshape(src_rows, width),
    )


def on_device(
    enc_hidden,
    mlp_gain,
    final_gain,
    w_gate,
    w_up,
    w_down,
    key_weight,
    value_weight,
    queries,
    context_grad,
):
    rows_contract = (((0,), (0,)), ((), ()))
    cols_contract = (((1,), (1,)), ((), ()))
    hidden_wide = enc_hidden.astype(jnp.float32)
    square_in = lax.psum(jnp.sum(hidden_wide * hidden_wide, axis=1), "section")
    inv_in = lax.rsqrt(square_in / D + EPSILON)[:, None]
    normed = (hidden_wide * inv_in * mlp_gain[None, :]).astype(jnp.bfloat16)
    normed_all = lax.all_gather(normed, "tensor", axis=0, tiled=True)
    picked = normed_all
    gate_part = jnp.dot(picked, w_gate, preferred_element_type=jnp.float32)
    up_part = jnp.dot(picked, w_up, preferred_element_type=jnp.float32)
    gate_up = lax.psum_scatter(
        jnp.concatenate([gate_part, up_part], axis=1), "section", scatter_dimension=0, tiled=True
    )
    hidden_width = w_gate.shape[1]
    gate_pre = gate_up[:, :hidden_width]
    up_pre = gate_up[:, hidden_width:]
    sigmoid_gate = jax.nn.sigmoid(gate_pre)
    activated = gate_pre * sigmoid_gate
    hidden_act = (activated * up_pre).astype(jnp.bfloat16)
    hidden_all = lax.all_gather(hidden_act, "section", axis=0, tiled=True)
    picked = hidden_all
    mixed = lax.psum_scatter(
        jnp.dot(picked, w_down, preferred_element_type=jnp.float32),
        "tensor",
        scatter_dimension=0,
        tiled=True,
    )
    outer = hidden_wide + mixed
    square_out = lax.psum(jnp.sum(outer * outer, axis=1), "section")
    inv_out = lax.rsqrt(square_out / D + EPSILON)[:, None]
    encoded = (outer * inv_out * final_gain[None, :]).astype(jnp.bfloat16)
    key_matrix = key_weight[0]
    value_matrix = value_weight[0]
    head_width = key_matrix.shape[1]
    encoded_feat = lax.all_gather(encoded, "section", axis=1, tiled=True)
    block_rows = lax.all_gather(encoded_feat, "tensor", axis=0, tiled=True)
    key_part = jnp.dot(block_rows, key_matrix, preferred_element_type=jnp.float32)
    value_part = jnp.dot(block_rows, value_matrix, preferred_element_type=jnp.float32)
    joined = jnp.concatenate([key_part, value_part], axis=1)
    keys_wide = joined[:, :head_width]
    values_wide = joined[:, head_width:]
    keys = keys_wide.astype(jnp.bfloat16)
    values = values_wide.astype(jnp.bfloat16)
    query_grad, key_grad, value_grad = attend(queries[0], context_grad[0], keys, values)
    total = lax.dot_general(key_grad, key_matrix, cols_contract, preferred_element_type=jnp.float32)
    partial_rows = lax.psum_scatter(
        total
        + lax.dot_general(
            value_grad, value_matrix, cols_contract, preferred_element_type=jnp.float32
        ),
        "tensor",
        scatter_dimension=0,
        tiled=True,
    )
    encoded_grad = lax.psum_scatter(partial_rows, "section", scatter_dimension=1, tiled=True)
    scaled_out = final_gain[None, :] * encoded_grad
    inner_out = lax.psum(jnp.sum(scaled_out * outer, axis=1), "section")
    outer_grad = (
        inv_out * scaled_out - outer * inv_out * inv_out * inv_out * (inner_out / D)[:, None]
    )
    outer_grad_bf = outer_grad.astype(jnp.bfloat16)
    outer_all = lax.all_gather(outer_grad_bf, "tensor", axis=0, tiled=True)
    down_weight_grad = lax.dot_general(
        hidden_all, outer_all, rows_contract, preferred_element_type=jnp.float32
    ).astype(jnp.bfloat16)
    picked = outer_all
    act_grad = lax.psum_scatter(
        lax.dot_general(picked, w_down, cols_contract, preferred_element_type=jnp.float32),
        "section",
        scatter_dimension=0,
        tiled=True,
    )
    up_grad = (act_grad * activated).astype(jnp.bfloat16)
    gate_grad = (act_grad * up_pre * sigmoid_gate * (1.0 + gate_pre * (1.0 - sigmoid_gate))).astype(
        jnp.bfloat16
    )
    gate_all, up_all = (
        lax.all_gather(gate_grad, "section", axis=0, tiled=True),
        lax.all_gather(up_grad, "section", axis=0, tiled=True),
    )
    gate_weight_grad = lax.dot_general(
        normed_all, gate_all, rows_contract, preferred_element_type=jnp.float32
    ).astype(jnp.bfloat16)
    up_weight_grad = lax.dot_general(
        normed_all, up_all, rows_contract, preferred_element_type=jnp.float32
    ).astype(jnp.bfloat16)
    total = lax.dot_general(gate_all, w_gate, cols_contract, preferred_element_type=jnp.float32)
    normed_grad = lax.psum_scatter(
        total + lax.dot_general(up_all, w_up, cols_contract, preferred_element_type=jnp.float32),
        "tensor",
        scatter_dimension=0,
        tiled=True,
    )
    scaled_in = mlp_gain[None, :] * normed_grad
    inner_in = lax.psum(jnp.sum(scaled_in * hidden_wide, axis=1), "section")
    hidden_grad = (
        outer_grad
        + inv_in * scaled_in
        - hidden_wide * inv_in * inv_in * inv_in * (inner_in / D)[:, None]
    )
    return (query_grad[None, :, :], hidden_grad, gate_weight_grad, up_weight_grad, down_weight_grad)


def solution(mesh):
    in_specs = (
        P(("dp", "tensor"), "section"),
        P("section"),
        P("section"),
        P("section", "tensor"),
        P("section", "tensor"),
        P("tensor", "section"),
        P("section", None, "tensor"),
        P("section", None, "tensor"),
        P("section", "dp", "tensor"),
        P("section", "dp", "tensor"),
    )
    out_specs = (
        P("section", "dp", "tensor"),
        P(("dp", "tensor"), "section"),
        P(("dp", "section"), "tensor"),
        P(("dp", "section"), "tensor"),
        P(("dp", "tensor"), "section"),
    )
    return jax.shard_map(
        on_device, mesh=mesh, in_specs=in_specs, out_specs=out_specs, check_vma=False
    )
```

profile of v0, /device:TPU:0, one launch (start us, length us, event | category | flops | bytes accessed | tf_op | source)
XLA Modules:
  0.0 318.8 jit_solution(16094628086690990987)
XLA Ops:
  8.2 13.5 %psum.28 = f32[16]{0:T(128)S(1)} all-reduce(f32[16]{0:T(128)S(1)} %fusion.58), channel_id=1, replica_groups=mesh['section'=4,'tensor'=4,'dp'=2] {'section'}, use_global_device_ids=true, to_apply=%region_1.0 | all-reduce | flops 16 | bytes 128 | tf_op jit(solution)/shard_map/psum | solution.py:66
  22.6 8.2 %all_gather.21 = bf16[64,512]{1,0:T(8,128)(2,1)S(1)} all-gather(bf16[16,512]{1,0:T(8,128)(2,1)S(1)} %fusion.54), channel_id=1, replica_groups=mesh['section'=4,'tensor'=4,'dp'=2] {'tensor'}, dimensions={0}, use_global_device_ids=true | all-gather | bytes 81920 | tf_op jit(solution)/shard_map/all_gather | solution.py:69
  34.5 24.6 %reduce-scatter.7.cloned.1.call-done = f32[16,4096]{1,0:T(8,128)} async-done(((f32[64,4096]{1,0:T(8,128)}), f32[16,4096]{1,0:T(8,128)}) %reduce-scatter.7.cloned.1.call-update) | async-done | bytes 262160 | tf_op jit(solution)/shard_map/reduce_scatter | solution.py:73
  60.2 14.3 %all_gather.22 = bf16[64,2048]{1,0:T(8,128)(2,1)S(1)} all-gather(bf16[16,2048]{1,0:T(8,128)(2,1)S(1)} %multiply_convert_fusion.2), channel_id=1, replica_groups=mesh['section'=4,'tensor'=4,'dp'=2] {'section'}, dimensions={0}, use_global_device_ids=true | all-gather | bytes 327680 | tf_op jit(solution)/shard_map/all_gather | solution.py:82
  75.7 4.5 %reshape_squeeze.6 = bf16[1024,4,256]{2,1,0:T(4,128)(2,1)} reshape(bf16[1,1024,1024]{2,1,0:T(8,128)(2,1)} %param.18) | data formatting | bytes 4194304 | tf_op jit(solution)/shard_map/reshape;squeeze | solution.py:18
  80.2 4.0 %copy.27 = bf16[1,1024,1024]{1,2,0:T(8,128)(2,1)} copy(bf16[1,1024,1024]{2,1,0:T(8,128)(2,1)} %param.19) | data formatting | bytes 4194304 | tf_op args[9]
  84.2 14.1 %reduce-scatter.9.cloned.1.call-done = f32[16,512]{1,0:T(8,128)} async-done(((f32[64,512]{1,0:T(8,128)}), f32[16,512]{1,0:T(8,128)}) %reduce-scatter.9.cloned.1.call-update) | async-done | bytes 32784 | tf_op jit(solution)/shard_map/reduce_scatter | solution.py:84
  99.1 11.8 %psum.29 = f32[16]{0:T(128)S(1)} all-reduce(f32[16]{0:T(128)S(1)} %multiply_reduce_fusion.1), channel_id=1, replica_groups=mesh['section'=4,'tensor'=4,'dp'=2] {'section'}, use_global_device_ids=true, to_apply=%region_5.0 | all-reduce | flops 16 | bytes 128 | tf_op jit(solution)/shard_map/psum | solution.py:91
  111.7 13.1 %all_gather.23 = bf16[16,2048]{1,0:T(8,128)(2,1)S(1)} all-gather(bf16[16,512]{1,0:T(8,128)(2,1)S(1)} %multiply_convert_fusion.3), channel_id=1, replica_groups=mesh['section'=4,'tensor'=4,'dp'=2] {'section'}, dimensions={1}, use_global_device_ids=true | all-gather | bytes 81920 | tf_op jit(solution)/shard_map/all_gather | solution.py:97
  124.9 8.8 %all_gather.24 = bf16[64,2048]{1,0:T(8,128)(2,1)S(1)} all-gather(bf16[16,2048]{1,0:T(8,128)(2,1)S(1)} %all_gather.23), channel_id=1, replica_groups=mesh['section'=4,'tensor'=4,'dp'=2] {'tensor'}, dimensions={0}, use_global_device_ids=true | all-gather | bytes 327680 | tf_op jit(solution)/shard_map/all_gather | solution.py:98
  133.7 3.8 %fusion.35 = bf16[64,1024]{1,0:T(8,128)(2,1)} fusion(bf16[64,2048]{1,0:T(8,128)(2,1)S(1)} %all_gather.24, bf16[1,2048,1024]{2,1,0:T(8,128)(2,1)} %param.17), kind=kOutput, calls=%fused_computation.31 | convolution fusion | flops 268500992 | bytes 4587520 | tf_op jit(solution)/shard_map/dot_general | solution.py:100
  141.1 3.0 fusion.38
  144.1 2.5 fusion.1
  147.7 2.6 fusion.28
  155.5 22.5 %reduce-scatter.11.cloned.1.call-done = f32[16,2048]{1,0:T(8,128)} async-done(((f32[64,2048]{1,0:T(8,128)}), f32[16,2048]{1,0:T(8,128)}) %reduce-scatter.11.cloned.1.call-update) | async-done | bytes 131088 | tf_op jit(solution)/shard_map/reduce_scatter | solution.py:108
  178.0 21.5 %reduce-scatter.13.cloned.1.call-done = f32[16,512]{1,0:T(8,128)} async-done(((f32[16,2048]{1,0:T(8,128)}), f32[16,512]{1,0:T(8,128)}) %reduce-scatter.13.cloned.1.call-update) | async-done | bytes 32784 | tf_op jit(solution)/shard_map/reduce_scatter | solution.py:117
  200.3 8.8 %psum.30 = f32[16]{0:T(128)S(1)} all-reduce(f32[16]{0:T(128)S(1)} %multiply_reduce_fusion), channel_id=1, replica_groups=mesh['section'=4,'tensor'=4,'dp'=2] {'section'}, use_global_device_ids=true, to_apply=%region_12.0 | all-reduce | flops 16 | bytes 128 | tf_op jit(solution)/shard_map/psum | solution.py:119
  210.0 8.3 %all_gather.25 = bf16[64,512]{1,0:T(8,128)(2,1)S(1)} all-gather(bf16[16,512]{1,0:T(8,128)(2,1)S(1)} %fusion.60), channel_id=1, replica_groups=mesh['section'=4,'tensor'=4,'dp'=2] {'tensor'}, dimensions={0}, use_global_device_ids=true | all-gather | bytes 81920 | tf_op jit(solution)/shard_map/all_gather | solution.py:124
  222.0 3.9 %copy.36 = bf16[1,1024,1024]{2,1,0:T(8,128)(2,1)} copy(bf16[1,1024,1024]{1,2,0:T(8,128)(2,1)} %bitcast.84) | data formatting | bytes 4194304
  228.0 12.1 %reduce-scatter.15.cloned.1.call-done = f32[16,2048]{1,0:T(8,128)} async-done(((f32[64,2048]{1,0:T(8,128)}), f32[16,2048]{1,0:T(8,128)}) %reduce-scatter.15.cloned.1.call-update) | async-done | bytes 131088 | tf_op jit(solution)/shard_map/reduce_scatter | solution.py:129
  241.0 14.1 %all_gather.27 = bf16[64,2048]{1,0:T(8,128)(2,1)S(1)} all-gather(bf16[16,2048]{1,0:T(8,128)(2,1)S(1)} %get-tuple-element.15), channel_id=1, replica_groups=mesh['section'=4,'tensor'=4,'dp'=2] {'section'}, dimensions={0}, use_global_device_ids=true | all-gather | bytes 327680 | tf_op jit(solution)/shard_map/all_gather | solution.py:141
  255.1 14.4 %all_gather.26 = bf16[64,2048]{1,0:T(8,128)(2,1)S(1)} all-gather(bf16[16,2048]{1,0:T(8,128)(2,1)S(1)} %get-tuple-element.16), channel_id=1, replica_groups=mesh['section'=4,'tensor'=4,'dp'=2] {'section'}, dimensions={0}, use_global_device_ids=true | all-gather | bytes 327680 | tf_op jit(solution)/shard_map/all_gather | solution.py:140
  277.5 20.4 %reduce-scatter.17.cloned.1.call-done = f32[16,512]{1,0:T(8,128)} async-done(((f32[64,512]{1,0:T(8,128)}), f32[16,512]{1,0:T(8,128)}) %reduce-scatter.17.cloned.1.call-update) | async-done | bytes 32784 | tf_op jit(solution)/shard_map/reduce_scatter | solution.py:150
  298.8 11.7 %psum.31 = f32[16]{0:T(128)S(1)} all-reduce(f32[16]{0:T(128)S(1)} %fusion.59), channel_id=1, replica_groups=mesh['section'=4,'tensor'=4,'dp'=2] {'section'}, use_global_device_ids=true, to_apply=%region_16.0 | all-reduce | flops 16 | bytes 128 | tf_op jit(solution)/shard_map/psum | solution.py:157
  (77 shorter events, 38.1 us)
Async XLA Ops:
  7.2 67.3 %copy-start = (bf16[2048,512]{1,0:T(8,128)(2,1)S(1)}, bf16[2048,512]{1,0:T(8,128)(2,1)}, u32[]{:S(2)}) copy-start(bf16[2048,512]{1,0:T(8,128)(2,1)} %param.15) | copy-start | bytes 6291460
  7.2 52.0 %reduce-scatter.7.cloned.1.call-start = ((), (), s32[]{:S(2)}) async-start(), calls=%async_computation.6 | async-start | bytes 1310720 | tf_op jit(solution)/shard_map/reduce_scatter | solution.py:73
  21.7 11.3 %copy-start.5 = (bf16[512,2048]{1,0:T(8,128)(2,1)S(1)}, bf16[512,2048]{1,0:T(8,128)(2,1)}, u32[]{:S(2)}) copy-start(bf16[512,2048]{1,0:T(8,128)(2,1)} %param.13) | copy-start | bytes 6291460
  34.5 63.7 %reduce-scatter.9.cloned.1.call-start = ((), (), s32[]{:S(2)}) async-start(), calls=%async_computation.7 | async-start | bytes 163840 | tf_op jit(solution)/shard_map/reduce_scatter | solution.py:84
  75.7 102.3 %reduce-scatter.11.cloned.1.call-start = ((), (), s32[]{:S(2)}) async-start(), calls=%async_computation.8 | async-start | bytes 655360 | tf_op jit(solution)/shard_map/reduce_scatter | solution.py:108
  80.2 18.0 %copy-start.11 = (bf16[16,512]{1,0:T(8,128)(2,1)S(1)}, bf16[16,512]{1,0:T(8,128)(2,1)}, u32[]{:S(2)}) copy-start(bf16[16,512]{1,0:T(8,128)(2,1)} %param.10) | copy-start | bytes 49156
  80.2 30.7 %copy-start.14 = (f32[512]{0:T(512)S(1)}, f32[512]{0:T(512)}, u32[]{:S(2)}) copy-start(f32[512]{0:T(512)} %param.12) | copy-start | bytes 6148
  133.7 3.8 %copy-start.2 = (bf16[1,2048,1024]{2,1,0:T(8,128)(2,1)S(1)}, bf16[1,2048,1024]{2,1,0:T(8,128)(2,1)}, u32[]{:S(2)}) copy-start(bf16[1,2048,1024]{2,1,0:T(8,128)(2,1)} %param.16) | copy-start | bytes 12582916
  137.5 1.6 copy-start.6
  138.4 2.7 copy-start.8
  146.6 3.7 %copy-start.7 = (bf16[1024,4,256]{2,1,0:T(4,128)(2,1)S(1)}, bf16[1024,4,256]{2,1,0:T(4,128)(2,1)}, u32[]{:S(2)}) copy-start(bf16[1024,4,256]{2,1,0:T(4,128)(2,1)} %reshape_squeeze.6) | copy-start | bytes 6291460
  147.7 3.3 %copy-start.1 = (bf16[1,2048,1024]{2,1,0:T(8,128)(2,1)S(1)}, bf16[1,2048,1024]{2,1,0:T(8,128)(2,1)}, u32[]{:S(2)}) copy-start(bf16[1,2048,1024]{2,1,0:T(8,128)(2,1)} %param.17) | copy-start | bytes 12582916
  151.0 2.2 copy-start.3
  153.2 46.3 %copy-start.12 = (f32[16,512]{1,0:T(8,128)S(1)}, f32[16,512]{1,0:T(8,128)}, u32[]{:S(2)}) copy-start(f32[16,512]{1,0:T(8,128)} %reduce-scatter.9.cloned.1.call-done) | copy-start | bytes 98308
  155.4 64.5 %copy-start.9 = (bf16[64,1024]{1,0:T(8,128)(2,1)S(1)}, bf16[64,1024]{1,0:T(8,128)(2,1)}, u32[]{:S(2)}) copy-start(bf16[64,1024]{1,0:T(8,128)(2,1)} %copy-done.8) | copy-start | bytes 393220
  155.4 44.1 %reduce-scatter.13.cloned.1.call-start = ((), (), s32[]{:S(2)}) async-start(), calls=%async_computation.9 | async-start | bytes 163840 | tf_op jit(solution)/shard_map/reduce_scatter | solution.py:117
  177.9 62.1 %reduce-scatter.15.cloned.1.call-start = ((), (), s32[]{:S(2)}) async-start(), calls=%async_computation.10 | async-start | bytes 655360 | tf_op jit(solution)/shard_map/reduce_scatter | solution.py:129
  219.9 78.0 %reduce-scatter.17.cloned.1.call-start = ((), (), s32[]{:S(2)}) async-start(), calls=%async_computation.11 | async-start | bytes 163840 | tf_op jit(solution)/shard_map/reduce_scatter | solution.py:150
  225.9 14.1 %copy-start.10 = (f32[16,4096]{1,0:T(8,128)S(1)}, f32[16,4096]{1,0:T(8,128)}, u32[]{:S(2)}) copy-start(f32[16,4096]{1,0:T(8,128)} %reduce-scatter.7.cloned.1.call-done) | copy-start | bytes 786436
  269.4 4.6 %copy-start.4 = (bf16[512,2048]{1,0:T(8,128)(2,1)S(1)}, bf16[512,2048]{1,0:T(8,128)(2,1)}, u32[]{:S(2)}) copy-start(bf16[512,2048]{1,0:T(8,128)(2,1)} %param.14) | copy-start | bytes 6291460
  274.0 23.9 %copy-start.15 = (f32[512]{0:T(512)S(1)}, f32[512]{0:T(512)}, u32[]{:S(2)}) copy-start(f32[512]{0:T(512)} %param.11) | copy-start | bytes 6148
  274.0 36.5 %copy-start.13 = (f32[16,512]{1,0:T(8,128)S(1)}, f32[16,512]{1,0:T(8,128)}, u32[]{:S(2)}) copy-start(f32[16,512]{1,0:T(8,128)} %reduce-scatter.13.cloned.1.call-done) | copy-start | bytes 98308
Sparse Core Ops, SparseCore 0:
  34.6 24.5 reduce-scatter.6
  75.8 22.4 reduce-scatter.8
  155.5 22.3 reduce-scatter.10
  180.0 19.4 reduce-scatter.12
  220.0 20.0 reduce-scatter.14
  275.6 22.2 reduce-scatter.16
where the time goes:
time: 320 us; the launch traced here: 319 us
  blocking collectives  127 us (40%)
  waiting for transfers between devices  115 us (36%)
  matrix products  35 us (11%)
  local copies, waits for them, and re-layouts  15.2 us (5%)
  between operations  14.2 us (4%)
  other arithmetic  11.9 us (4%)
    reduce_scatter x1, waiting for transfers between devices, on_device(): lax.psum_scatter(jnp.concatenate([gate_part, up_part], axis=1), 'section'...  24.6 us
    reduce_scatter x1, waiting for transfers between devices, on_device(): lax.psum_scatter(total + lax.dot_general(value_grad, value_matrix, cols_c...  22.5 us
    reduce_scatter x1, waiting for transfers between devices, on_device(): lax.psum_scatter(partial_rows, 'section', scatter_dimension=1, tiled=True)  21.5 us
    reduce_scatter x1, waiting for transfers between devices, on_device(): lax.psum_scatter(total + lax.dot_general(up_all, w_up, cols_contract, pre...  20.4 us
    all_gather x1, blocking collectives, on_device(): lax.all_gather(gate_grad, 'section', axis=0, tiled=True)  14.4 us
    all_gather x1, blocking collectives, on_device(): hidden_all = lax.all_gather(hidden_act, 'section', axis=0, tiled=True)  14.3 us
    reduce_scatter x1, waiting for transfers between devices, on_device(): lax.psum_scatter(jnp.dot(picked, w_down, preferred_element_type=jnp.float...  14.1 us
    all_gather x1, blocking collectives, on_device(): lax.all_gather(up_grad, 'section', axis=0, tiled=True)  14.1 us
  transfers between devices with their start and end apart: 6, of which 6 were waited for; matrix products, arithmetic and copies ran while one was open for 6% of the time, Pallas kernels for 0%

commit v1 on v0

v1 whole, which is shorter than its diff:
```python
import functools
import jax
import jax.numpy as jnp
from jax import lax
from jax.experimental import pallas as pl
from jax.experimental.pallas import tpu as pltpu
from jax.sharding import PartitionSpec as P

HEAD = 256
EPSILON = 1e-06
LANES = 128
MESH = pl.DeviceIdType.MESH
VMEM_LIMIT = 40 * 1024 * 1024
ROWS = (((0,), (0,)), ((), ()))
COLS = (((1,), (1,)), ((), ()))
F32 = jnp.float32
BF16 = jnp.bfloat16


def enter(sizes):
    barrier = pltpu.get_barrier_semaphore()
    for axis, n in sizes:
        me = lax.axis_index(axis)
        for k in range(1, n):
            pl.semaphore_signal(
                barrier, inc=1, device_id={axis: lax.rem(me + k, n)}, device_id_type=MESH
            )
    pl.semaphore_wait(barrier, sum(n - 1 for _, n in sizes))


def post(axis, n, source, target, send_sem, recv_sem):
    me = lax.axis_index(axis)
    copies = []
    for k in range(1, n):
        peer = lax.rem(me + k, n)
        copy = pltpu.make_async_remote_copy(
            src_ref=source(peer),
            dst_ref=target(k - 1),
            send_sem=send_sem.at[k - 1],
            recv_sem=recv_sem.at[k - 1],
            device_id={axis: peer},
            device_id_type=MESH,
        )
        copy.start()
        copies.append(copy)
    return copies


def gather(axis, n, ref, send_sem, recv_sem):
    me = lax.axis_index(axis)
    return post(axis, n, lambda peer: ref.at[me], lambda k: ref.at[me], send_sem, recv_sem)


def scatter(axis, n, out, into, send_sem, recv_sem):
    return post(axis, n, lambda peer: out.at[peer], lambda k: into.at[k], send_sem, recv_sem)


def finish(*groups):
    for copies in groups:
        for copy in copies:
            copy.wait()


def total(own, into, n):
    acc = own.astype(F32)
    for k in range(n - 1):
        acc = acc + into[k].astype(F32)
    return acc


def forward_kernel(
    S, N, x_ref, mg_ref, fg_ref, wg_hbm, wu_hbm, wd_hbm,
    enc_out, hid_out, normed_out, act_out, fac_out, inv_in_out, inv_out_out, outer_out,
    wg, wu, wd, xg, sqs, sqr, gus, gur, hid_all, inv_all, ds, dr, feat, sqo, enc,
    load_sem, ssem, rsem,
):
    tt, F = x_ref.shape
    T = N * tt
    ts = T // S
    H = wg.shape[1]
    D = F * S
    sec = lax.axis_index("section")
    ten = lax.axis_index("tensor")
    loads = [
        pltpu.make_async_copy(src, dst, load_sem.at[i])
        for i, (src, dst) in enumerate(((wg_hbm, wg), (wu_hbm, wu), (wd_hbm, wd)))
    ]
    for load in loads:
        load.start()
    xg[ten] = x_ref[...]
    enter((("section", S), ("tensor", N)))
    finish(post("tensor", N, lambda p: x_ref, lambda k: xg.at[ten], ssem.at[0], rsem.at[0]))
    wide = xg[...].reshape(T, F).astype(F32)
    scaled = (wide * mg_ref[...]).astype(BF16)
    square = jnp.sum(wide * wide, axis=1, keepdims=True)
    sqs[...] = jnp.broadcast_to(square, (T, LANES)).reshape(S, ts, LANES)
    loads[0].wait()
    gus[0] = jnp.dot(scaled, wg[...], preferred_element_type=F32).astype(BF16).reshape(S, ts, H)
    move_g = scatter("section", S, gus.at[0], gur.at[0], ssem.at[1], rsem.at[1])
    move_q = scatter("section", S, sqs, sqr, ssem.at[3], rsem.at[3])
    loads[1].wait()
    gus[1] = jnp.dot(scaled, wu[...], preferred_element_type=F32).astype(BF16).reshape(S, ts, H)
    move_u = scatter("section", S, gus.at[1], gur.at[1], ssem.at[2], rsem.at[2])
    finish(move_g, move_q)
    inv = lax.rsqrt(total(sqs[sec], sqr, S) / D + EPSILON)
    inv_all[sec] = inv
    move_i = gather("section", S, inv_all, ssem.at[5], rsem.at[5])
    inv = inv[:, :1]
    gate_pre = total(gus[0, sec], gur.at[0], S) * inv
    sig = jax.nn.sigmoid(gate_pre)
    act = gate_pre * sig
    act_out[...] = act
    slope = sig * (1.0 + gate_pre * (1.0 - sig))
    finish(move_u)
    up_pre = total(gus[1, sec], gur.at[1], S) * inv
    hid_all[sec] = (act * up_pre).astype(BF16)
    move_h = gather("section", S, hid_all, ssem.at[4], rsem.at[4])
    fac_out[...] = up_pre * slope
    finish(move_i)
    inv_tok = inv_all[...].reshape(T, LANES)
    normed_out[...] = (wide * inv_tok[:, :1] * mg_ref[...]).astype(BF16)
    inv_flat = inv_all.reshape(T, LANES)
    inv_in_out[...] = inv_flat[pl.ds(pl.multiple_of(ten * tt, tt), tt), :]
    loads[2].wait()
    finish(move_h)
    hid = hid_all[...].reshape(T, H)
    ds[...] = jnp.dot(hid, wd[...], preferred_element_type=F32).astype(BF16).reshape(N, tt, F)
    move_d = scatter("tensor", N, ds, dr, ssem.at[6], rsem.at[6])
    hid_out[...] = hid
    finish(move_d)
    outer = x_ref[...].astype(F32) + total(ds[ten], dr, N)
    outer_out[...] = outer
    feat[sec] = (outer * fg_ref[...]).astype(BF16)
    sqo[sec] = jnp.broadcast_to(jnp.sum(outer * outer, axis=1, keepdims=True), (tt, LANES))
    move_s = gather("section", S, sqo, ssem.at[8], rsem.at[8])
    move_f = gather("section", S, feat, ssem.at[7], rsem.at[7])
    finish(move_s, move_f)
    inv_o = lax.rsqrt(jnp.sum(sqo[...], axis=0) / D + EPSILON)
    inv_out_out[...] = inv_o
    enc[ten] = (feat[...].astype(F32) * inv_o[None, :, :1]).astype(BF16)
    finish(gather("tensor", N, enc, ssem.at[9], rsem.at[9]))
    enc_out[...] = enc[...]


def attention_kernel(S, N, enc_ref, wk_ref, wv_ref, q_ref, c_ref, qg_ref, eg_ref, acc):
    step = pl.program_id(0)
    tt, F = enc_ref.shape[2:]
    T = N * tt
    scale = HEAD ** (-0.5)
    keys = jnp.zeros((T, HEAD), F32)
    values = jnp.zeros((T, HEAD), F32)
    for s in range(S):
        block = enc_ref[:, s].reshape(T, F)
        keys += jnp.dot(block, wk_ref[s * F : (s + 1) * F, :], preferred_element_type=F32)
        values += jnp.dot(block, wv_ref[s * F : (s + 1) * F, :], preferred_element_type=F32)
    keys = keys.astype(BF16)
    values = values.astype(BF16)
    q = q_ref[...]
    c = c_ref[...]
    scores = lax.dot_general(keys, q, COLS, preferred_element_type=F32) * scale
    weights = jnp.exp(scores - jnp.max(scores, axis=0, keepdims=True))
    probs = weights / jnp.sum(weights, axis=0, keepdims=True)
    probs_bf = probs.astype(BF16)
    dprob = lax.dot_general(values, c, COLS, preferred_element_type=F32)
    delta = jnp.sum(probs_bf.astype(F32) * dprob, axis=0, keepdims=True)
    dscore = (probs * (dprob - delta) * scale).astype(BF16)
    qg_ref[...] = lax.dot_general(dscore, keys, ROWS, preferred_element_type=F32).astype(BF16)
    key_grad = jnp.dot(dscore, q, preferred_element_type=F32).astype(BF16)
    value_grad = jnp.dot(probs_bf, c, preferred_element_type=F32).astype(BF16)
    for s in range(S):
        rows = slice(s * F, (s + 1) * F)
        part = lax.dot_general(key_grad, wk_ref[rows, :], COLS, preferred_element_type=F32)
        part += lax.dot_general(value_grad, wv_ref[rows, :], COLS, preferred_element_type=F32)

        @pl.when(step == 0)
        def _():
            acc[s] = part

        @pl.when(step > 0)
        def _():
            acc[s] += part

    @pl.when(step == pl.num_programs(0) - 1)
    def _():
        for s in range(S):
            eg_ref[:, s] = acc[s].astype(BF16).reshape(N, tt, F)


def backward_kernel(
    S, N, eg_ref, x_ref, mg_ref, fg_ref, act_ref, fac_ref, inv_in_ref, inv_out_ref, outer_ref,
    wg_hbm, wu_hbm, wd_hbm,
    hg_out, oall_out, gate_out, up_out,
    wg, wu, wd, r6, s6, r6b, pin, oall, s9, r9, ggu, s11, r11, pin2,
    load_sem, ssem, rsem,
):
    tt, F = x_ref.shape
    T = N * tt
    ts = T // S
    H = wg.shape[1]
    D = F * S
    sec = lax.axis_index("section")
    ten = lax.axis_index("tensor")
    loads = [
        pltpu.make_async_copy(src, dst, load_sem.at[i])
        for i, (src, dst) in enumerate(((wd_hbm, wd), (wg_hbm, wg), (wu_hbm, wu)))
    ]
    for load in loads:
        load.start()
    enter((("section", S), ("tensor", N)))
    finish(scatter("tensor", N, eg_ref, r6, ssem.at[0], rsem.at[0]))
    s6[...] = total(eg_ref[ten], r6, N).astype(BF16)
    finish(scatter("section", S, s6, r6b, ssem.at[1], rsem.at[1]))
    outer = outer_ref[...]
    scaled_out = fg_ref[...] * total(s6[sec], r6b, S)
    pin[sec] = jnp.broadcast_to(
        jnp.sum(scaled_out * outer, axis=1, keepdims=True), (tt, LANES)
    )
    finish(gather("section", S, pin, ssem.at[2], rsem.at[2]))
    inner = jnp.sum(pin[...], axis=0)[:, :1] / D
    inv_o = inv_out_ref[:, :1]
    outer_grad = inv_o * scaled_out - outer * (inv_o * inv_o * inv_o * inner)
    oall[ten] = outer_grad.astype(BF16)
    finish(gather("tensor", N, oall, ssem.at[3], rsem.at[3]))
    grads = oall[...].reshape(T, F)
    loads[0].wait()
    s9[...] = (
        lax.dot_general(grads, wd[...], COLS, preferred_element_type=F32)
        .astype(BF16)
        .reshape(S, ts, H)
    )
    move_a = scatter("section", S, s9, r9, ssem.at[4], rsem.at[4])
    oall_out[...] = grads
    finish(move_a)
    act_grad = total(s9[sec], r9, S)
    ggu[0, sec] = (act_grad * fac_ref[...]).astype(BF16)
    move_g = gather("section", S, ggu.at[0], ssem.at[5], rsem.at[5])
    ggu[1, sec] = (act_grad * act_ref[...]).astype(BF16)
    move_u = gather("section", S, ggu.at[1], ssem.at[6], rsem.at[6])
    loads[1].wait()
    finish(move_g)
    gate_all = ggu[0].reshape(T, H)
    gate_out[...] = gate_all
    part = lax.dot_general(gate_all, wg[...], COLS, preferred_element_type=F32)
    loads[2].wait()
    finish(move_u)
    up_all = ggu[1].reshape(T, H)
    part += lax.dot_general(up_all, wu[...], COLS, preferred_element_type=F32)
    s11[...] = part.astype(BF16).reshape(N, tt, F)
    move_n = scatter("tensor", N, s11, r11, ssem.at[7], rsem.at[7])
    up_out[...] = up_all
    finish(move_n)
    hidden = x_ref[...].astype(F32)
    scaled_in = mg_ref[...] * total(s11[ten], r11, N)
    pin2[sec] = jnp.broadcast_to(
        jnp.sum(scaled_in * hidden, axis=1, keepdims=True), (tt, LANES)
    )
    finish(gather("section", S, pin2, ssem.at[8], rsem.at[8]))
    inner_in = jnp.sum(pin2[...], axis=0)[:, :1] / D
    inv_in = inv_in_ref[:, :1]
    hg_out[...] = (
        outer_grad + inv_in * scaled_in - hidden * (inv_in * inv_in * inv_in * inner_in)
    )


def on_device(
    S, N, enc_hidden, mlp_gain, final_gain, w_gate, w_up, w_down, key_weight, value_weight,
    queries, context_grad,
):
    tt, F = enc_hidden.shape
    T = N * tt
    ts = T // S
    H = w_gate.shape[1]
    peers = max(S, N) - 1
    vmem = pl.BlockSpec(memory_space=pltpu.VMEM)
    hbm = pl.BlockSpec(memory_space=pl.ANY)
    shape = jax.ShapeDtypeStruct
    dma = pltpu.SemaphoreType.DMA
    mg = mlp_gain[None, :]
    fg = final_gain[None, :]
    weights = [pltpu.VMEM(w_gate.shape, BF16), pltpu.VMEM(w_up.shape, BF16),
               pltpu.VMEM(w_down.shape, BF16)]
    enc, hid, normed, act, fac, inv_in, inv_out, outer = pl.pallas_call(
        functools.partial(forward_kernel, S, N),
        out_shape=[
            shape((N, S, tt, F), BF16), shape((T, H), BF16), shape((T, F), BF16),
            shape((ts, H), F32), shape((ts, H), F32), shape((tt, LANES), F32),
            shape((tt, LANES), F32), shape((tt, F), F32),
        ],
        in_specs=[vmem] * 3 + [hbm] * 3,
        out_specs=[vmem] * 8,
        scratch_shapes=weights + [
            pltpu.VMEM((N, tt, F), BF16),
            pltpu.VMEM((S, ts, LANES), F32),
            pltpu.VMEM((S - 1, ts, LANES), F32),
            pltpu.VMEM((2, S, ts, H), BF16),
            pltpu.VMEM((2, S - 1, ts, H), BF16),
            pltpu.VMEM((S, ts, H), BF16),
            pltpu.VMEM((S, ts, LANES), F32),
            pltpu.VMEM((N, tt, F), BF16),
            pltpu.VMEM((N - 1, tt, F), BF16),
            pltpu.VMEM((S, tt, F), BF16),
            pltpu.VMEM((S, tt, LANES), F32),
            pltpu.VMEM((N, S, tt, F), BF16),
            dma((3,)), dma((10, peers)), dma((10, peers)),
        ],
        compiler_params=pltpu.CompilerParams(
            collective_id=0, has_side_effects=True, vmem_limit_bytes=VMEM_LIMIT
        ),
    )(enc_hidden, mg, fg, w_gate, w_up, w_down)

    wk, wv, q, c = key_weight[0], value_weight[0], queries[0], context_grad[0]
    D = wk.shape[0]
    rows = q.shape[0]
    heads = q.shape[1] // HEAD
    column = lambda depth: pl.BlockSpec((depth, HEAD), lambda h: (0, h))
    whole = pl.BlockSpec((N, S, tt, F), lambda h: (0, 0, 0, 0))
    query_grad, eg = pl.pallas_call(
        functools.partial(attention_kernel, S, N),
        grid=(heads,),
        out_shape=[shape(q.shape, BF16), shape((N, S, tt, F), BF16)],
        in_specs=[whole, column(D), column(D), column(rows), column(rows)],
        out_specs=[column(rows), whole],
        scratch_shapes=[pltpu.VMEM((S, T, F), F32)],
        compiler_params=pltpu.CompilerParams(
            dimension_semantics=("arbitrary",), vmem_limit_bytes=VMEM_LIMIT
        ),
    )(enc, wk, wv, q, c)

    hidden_grad, outer_all, gate_all, up_all = pl.pallas_call(
        functools.partial(backward_kernel, S, N),
        out_shape=[shape((tt, F), F32), shape((T, F), BF16), shape((T, H), BF16),
                   shape((T, H), BF16)],
        in_specs=[vmem] * 9 + [hbm] * 3,
        out_specs=[vmem] * 4,
        scratch_shapes=weights + [
            pltpu.VMEM((N - 1, S, tt, F), BF16),
            pltpu.VMEM((S, tt, F), BF16),
            pltpu.VMEM((S - 1, tt, F), BF16),
            pltpu.VMEM((S, tt, LANES), F32),
            pltpu.VMEM((N, tt, F), BF16),
            pltpu.VMEM((S, ts, H), BF16),
            pltpu.VMEM((S - 1, ts, H), BF16),
            pltpu.VMEM((2, S, ts, H), BF16),
            pltpu.VMEM((N, tt, F), BF16),
            pltpu.VMEM((N - 1, tt, F), BF16),
            pltpu.VMEM((S, tt, LANES), F32),
            dma((3,)), dma((9, peers)), dma((9, peers)),
        ],
        compiler_params=pltpu.CompilerParams(
            collective_id=1, has_side_effects=True, vmem_limit_bytes=VMEM_LIMIT
        ),
    )(eg, enc_hidden, mg, fg, act, fac, inv_in, inv_out, outer, w_gate, w_up, w_down)

    outer_product = lambda a, b: lax.dot_general(
        a, b, ROWS, preferred_element_type=F32
    ).astype(BF16)
    return (
        query_grad[None, :, :],
        hidden_grad,
        outer_product(normed, gate_all),
        outer_product(normed, up_all),
        outer_product(hid, outer_all),
    )


def solution(mesh):
    in_specs = (
        P(("dp", "tensor"), "section"),
        P("section"),
        P("section"),
        P("section", "tensor"),
        P("section", "tensor"),
        P("tensor", "section"),
        P("section", None, "tensor"),
        P("section", None, "tensor"),
        P("section", "dp", "tensor"),
        P("section", "dp", "tensor"),
    )
    out_specs = (
        P("section", "dp", "tensor"),
        P(("dp", "tensor"), "section"),
        P(("dp", "section"), "tensor"),
        P(("dp", "section"), "tensor"),
        P(("dp", "tensor"), "section"),
    )
    body = functools.partial(on_device, mesh.shape["section"], mesh.shape["tensor"])
    return jax.shard_map(
        body, mesh=mesh, in_specs=in_specs, out_specs=out_specs, check_vma=False
    )
```

time: 320 us -> 116 us (0.36)
  blocking collectives: 127 us -> 0 us
  waiting for transfers between devices: 115 us -> 0 us
  Pallas kernels: 0 us -> 97.5 us
  matrix products: 35 us -> 6.15 us
  between operations: 14.2 us -> 0.7 us
  other arithmetic: 11.9 us -> 0 us
  local copies, waits for them, and re-layouts: 15.2 us -> 11.3 us
    reduce_scatter x6 -> x0, waiting for transfers between devices: 115 us -> none  [the longest x1 24.6 us: on_device(): lax.psum_scatter(jnp.concatenate([gate_part, up_part], axis=1), 'section'...]
    pallas_call x0 -> x3, Pallas kernels: none -> 97.5 us  [the longest x1 43.7 us: on_device(): pl.pallas_call(functools.partial(backward_kernel, S, N), out_shape=[shape...]
    all_gather x7 -> x0, blocking collectives: 81.1 us -> none  [the longest x1 14.4 us: on_device(): lax.all_gather(gate_grad, 'section', axis=0, tiled=True)]
    psum x4 -> x0, blocking collectives: 45.8 us -> none  [the longest x1 13.5 us: on_device(): square_in = lax.psum(jnp.sum(hidden_wide * hidden_wide, axis=1), 'section')]
    dot_general x19 -> x3, matrix products: 35 us -> 6.15 us  [on_device(): lax.dot_general(a, b, ROWS, preferred_element_type=F32).astype(BF16)]
    convert_element_type x5 -> x0, other arithmetic: 4.61 us -> none  [the longest x1 1.01 us: on_device(): hidden_act = (activated * up_pre).astype(jnp.bfloat16)]
    another operation x1 -> x0, local copies, waits for them, and re-layouts: 4.5 us -> none  [attend(): query_heads = query_block.reshape(tgt_rows, heads_here, HEAD)]
    reduce_sum x4 -> x0, other arithmetic: 3.6 us -> none  [the longest x1 0.97 us: on_device(): square_in = lax.psum(jnp.sum(hidden_wide * hidden_wide, axis=1), 'section')]
  transfers between devices with their start and end apart: 6 -> 0, of which waited for: 6 -> 0; matrix products, arithmetic and copies ran while one was open for 6% -> 0% of each run, Pallas kernels for 0% -> 0%
where the time goes in v1:
time: 116 us
  Pallas kernels  97.5 us (84%)
  local copies, waits for them, and re-layouts  11.3 us (10%)
  matrix products  6.15 us (5%)
    pallas_call x1, Pallas kernels, on_device(): pl.pallas_call(functools.partial(backward_kernel, S, N), out_shape=[shape...  43.7 us
    pallas_call x1, Pallas kernels, on_device(): pl.pallas_call(functools.partial(forward_kernel, S, N), out_shape=[shape(...  41.9 us
    pallas_call x1, Pallas kernels, on_device(): pl.pallas_call(functools.partial(attention_kernel, S, N), grid=(heads,),...  11.9 us
    unnamed x27, local copies, waits for them, and re-layouts  11.3 us
    dot_general x3, matrix products, on_device(): lax.dot_general(a, b, ROWS, preferred_element_type=F32).astype(BF16)  6.15 us

profile of v1, /device:TPU:0, one launch (start us, length us, event | category | flops | bytes accessed | tf_op | source)
XLA Modules:
  0.0 115.6 jit_solution(7209333659417097259)
XLA Ops:
  0.6 0.0 copy-start
  0.6 1.6 %copy-done = bf16[512,2048]{1,0:T(8,128)(2,1)S(1)} copy-done((bf16[512,2048]{1,0:T(8,128)(2,1)S(1)}, bf16[512,2048]{1,0:T(8,128)(2,1)}, u32[]{:S(2)}) %copy-start) | copy-done | bytes 2097176
  2.2 0.0 copy-start.2
  2.2 1.6 %copy-done.2 = bf16[512,2048]{1,0:T(8,128)(2,1)S(1)} copy-done((bf16[512,2048]{1,0:T(8,128)(2,1)S(1)}, bf16[512,2048]{1,0:T(8,128)(2,1)}, u32[]{:S(2)}) %copy-start.2) | copy-done | bytes 2097176
  3.8 1.6 %copy-done.4 = bf16[2048,512]{1,0:T(8,128)(2,1)S(1)} copy-done((bf16[2048,512]{1,0:T(8,128)(2,1)S(1)}, bf16[2048,512]{1,0:T(8,128)(2,1)}, u32[]{:S(2)}) %copy-start.4) | copy-done | bytes 2097176
  5.4 0.0 copy-start.10
  5.4 0.7 copy-done.10
  6.1 0.7 copy-done.11
  6.8 0.7 copy-done.12
  7.5 41.9 %shard_map.137 = (bf16[4,4,16,512]{3,2,1,0:T(8,128)(2,1)S(1)}, bf16[64,2048]{1,0:T(8,128)(2,1)S(1)}, bf16[64,512]{1,0:T(8,128)(2,1)S(1)}, f32[16,2048]{1,0:T(8,1...) custom-call(bf16[16,512]{1,0:T(8,128)(2,1)S(1)} %copy-done.10, ...), custom_call_target="tpu_custom_call" | custom-call | tf_op jit(solution)/shard_map/pallas_call | solution.py:282
  49.4 0.0 copy-done.6
  49.4 0.0 copy-done.8
  49.4 0.0 copy-start.7
  49.5 2.2 %copy-done.7 = bf16[1,2048,1024]{2,1,0:T(8,128)(2,1)S(1)} copy-done((bf16[1,2048,1024]{2,1,0:T(8,128)(2,1)S(1)}, bf16[1,2048,1024]{2,1,0:T(8,128)(2,1)}, u32[]{:S(2)}) %copy-start.7) | copy-done | bytes 4194328
  51.6 1.6 %copy-done.9 = bf16[1,1024,1024]{2,1,0:T(8,128)(2,1)S(1)} copy-done((bf16[1,1024,1024]{2,1,0:T(8,128)(2,1)S(1)}, bf16[1,1024,1024]{2,1,0:T(8,128)(2,1)}, u32[]{:S(2)}) %copy-start.9) | copy-done | bytes 2097176
  53.2 11.9 %shard_map.138 = (bf16[1024,1024]{1,0:T(8,128)(2,1)}, bf16[4,4,16,512]{3,2,1,0:T(8,128)(2,1)S(1)}) custom-call(bf16[4,4,16,512]{3,2,1,0:T(8,128)(2,1)S(1)} %get-tuple-element.19.enc_ref, bf16[2048,1024]{1,0:T(8,128)(2,1)S(1)} %bitcast.13, bf16[2048,1024]{1,0:T(8,128)(2,1)S(1)} %bitcast.14, bf16[1024,1024]{1,0:T(8,128)(2,1)S(1)} %bitcast.15, ...), custom_call_target="tpu_custom_call" | custom-call | tf_op jit(solution)/shard_map/pallas_call | solution.py:317
  65.1 0.0 copy-done.1
  65.1 0.0 copy-done.3
  65.1 0.0 copy-done.5
  65.1 43.7 %shard_map.139 = (f32[16,512]{1,0:T(8,128)S(1)}, bf16[64,512]{1,0:T(8,128)(2,1)S(1)}, bf16[64,2048]{1,0:T(8,128)(2,1)S(1)}, bf16[64,2048]{1,0:T(8,128)(2,1)S(1)}) custom-call(bf16[4,4,16,512]{3,2,1,0:T(8,128)(2,1)S(1)} %get-tuple-element.21.eg_ref, bf16[16,512]{1,0:T(8,128)(2,1)S(1)} %copy-done.10, f32[1,512]{1,0:T(1,128)S(1)} %bitcast.18, ...), custom_call_target="tpu_custom_call" | custom-call | tf_op jit(solution)/shard_map/pallas_call | solution.py:329
  108.9 2.1 %convolution_convert_fusion = bf16[2048,512]{1,0:T(8,128)(2,1)} fusion(bf16[64,2048]{1,0:T(8,128)(2,1)S(1)} %get-tuple-element.31, bf16[64,512]{1,0:T(8,128)(2,1)S(1)} %get-tuple-element.32), kind=kOutput, calls=%fused_computation | convolution fusion | flops 135266304 | bytes 2424832 | tf_op jit(solution)/shard_map/dot_general | solution.py:354
  110.9 2.0 %convolution_convert_fusion.2 = bf16[512,2048]{1,0:T(8,128)(2,1)} fusion(bf16[64,512]{1,0:T(8,128)(2,1)S(1)} %get-tuple-element.28, bf16[64,2048]{1,0:T(8,128)(2,1)S(1)} %get-tuple-element.29), kind=kOutput, calls=%fused_computation.2 | convolution fusion | flops 135266304 | bytes 2424832 | tf_op jit(solution)/shard_map/dot_general | solution.py:354
  113.0 2.0 %convolution_convert_fusion.1 = bf16[512,2048]{1,0:T(8,128)(2,1)} fusion(bf16[64,512]{1,0:T(8,128)(2,1)S(1)} %get-tuple-element.28, bf16[64,2048]{1,0:T(8,128)(2,1)S(1)} %get-tuple-element.30), kind=kOutput, calls=%fused_computation.1 | convolution fusion | flops 135266304 | bytes 2424832 | tf_op jit(solution)/shard_map/dot_general | solution.py:354
  115.0 0.6 copy.16
  (9 shorter events, 0.0 us)
Async XLA Ops:
  0.6 1.6 %copy-start = (bf16[512,2048]{1,0:T(8,128)(2,1)S(1)}, bf16[512,2048]{1,0:T(8,128)(2,1)}, u32[]{:S(2)}) copy-start(bf16[512,2048]{1,0:T(8,128)(2,1)} %wg_hbm.3) | copy-start | bytes 6291460
  2.2 1.6 %copy-start.2 = (bf16[512,2048]{1,0:T(8,128)(2,1)S(1)}, bf16[512,2048]{1,0:T(8,128)(2,1)}, u32[]{:S(2)}) copy-start(bf16[512,2048]{1,0:T(8,128)(2,1)} %wu_hbm.3) | copy-start | bytes 6291460
  3.8 1.6 %copy-start.4 = (bf16[2048,512]{1,0:T(8,128)(2,1)S(1)}, bf16[2048,512]{1,0:T(8,128)(2,1)}, u32[]{:S(2)}) copy-start(bf16[2048,512]{1,0:T(8,128)(2,1)} %wd_hbm.3) | copy-start | bytes 6291460
  5.4 0.7 copy-start.10
  6.1 0.7 copy-start.11
  6.8 0.7 copy-start.12
  7.5 41.9 %copy-start.6 = (bf16[1,2048,1024]{2,1,0:T(8,128)(2,1)S(1)}, bf16[1,2048,1024]{2,1,0:T(8,128)(2,1)}, u32[]{:S(2)}) copy-start(bf16[1,2048,1024]{2,1,0:T(8,128)(2,1)} %param.16) | copy-start | bytes 12582916
  7.5 41.9 %copy-start.8 = (bf16[1,1024,1024]{2,1,0:T(8,128)(2,1)S(1)}, bf16[1,1024,1024]{2,1,0:T(8,128)(2,1)}, u32[]{:S(2)}) copy-start(bf16[1,1024,1024]{2,1,0:T(8,128)(2,1)} %param.18) | copy-start | bytes 6291460
  49.4 2.2 %copy-start.7 = (bf16[1,2048,1024]{2,1,0:T(8,128)(2,1)S(1)}, bf16[1,2048,1024]{2,1,0:T(8,128)(2,1)}, u32[]{:S(2)}) copy-start(bf16[1,2048,1024]{2,1,0:T(8,128)(2,1)} %param.17) | copy-start | bytes 12582916
  51.6 1.6 %copy-start.9 = (bf16[1,1024,1024]{2,1,0:T(8,128)(2,1)S(1)}, bf16[1,1024,1024]{2,1,0:T(8,128)(2,1)}, u32[]{:S(2)}) copy-start(bf16[1,1024,1024]{2,1,0:T(8,128)(2,1)} %param.19) | copy-start | bytes 6291460
  53.2 11.9 %copy-start.1 = (bf16[512,2048]{1,0:T(8,128)(2,1)S(1)}, bf16[512,2048]{1,0:T(8,128)(2,1)}, u32[]{:S(2)}) copy-start(bf16[512,2048]{1,0:T(8,128)(2,1)} %wg_hbm.3) | copy-start | bytes 6291460
  53.2 11.9 %copy-start.3 = (bf16[512,2048]{1,0:T(8,128)(2,1)S(1)}, bf16[512,2048]{1,0:T(8,128)(2,1)}, u32[]{:S(2)}) copy-start(bf16[512,2048]{1,0:T(8,128)(2,1)} %wu_hbm.3) | copy-start | bytes 6291460
  53.2 11.9 %copy-start.5 = (bf16[2048,512]{1,0:T(8,128)(2,1)S(1)}, bf16[2048,512]{1,0:T(8,128)(2,1)}, u32[]{:S(2)}) copy-start(bf16[2048,512]{1,0:T(8,128)(2,1)} %wd_hbm.3) | copy-start | bytes 6291460

commit v2 on v1

v2 whole, which is shorter than its diff:
```python
import functools
import jax
import jax.numpy as jnp
from jax import lax
from jax.experimental import pallas as pl
from jax.experimental.pallas import tpu as pltpu
from jax.sharding import PartitionSpec as P

HEAD = 256
EPSILON = 1e-06
LANES = 128
MESH = pl.DeviceIdType.MESH
VMEM_LIMIT = 58 * 1024 * 1024
ROWS = (((0,), (0,)), ((), ()))
COLS = (((1,), (1,)), ((), ()))
F32 = jnp.float32
BF16 = jnp.bfloat16


def enter(sizes):
    barrier = pltpu.get_barrier_semaphore()
    for axis, n in sizes:
        me = lax.axis_index(axis)
        for k in range(1, n):
            pl.semaphore_signal(
                barrier, inc=1, device_id={axis: lax.rem(me + k, n)}, device_id_type=MESH
            )
    pl.semaphore_wait(barrier, sum(n - 1 for _, n in sizes))


def post(axis, n, source, target, send_sem, recv_sem):
    me = lax.axis_index(axis)
    copies = []
    for k in range(1, n):
        peer = lax.rem(me + k, n)
        copy = pltpu.make_async_remote_copy(
            src_ref=source(peer),
            dst_ref=target(k - 1),
            send_sem=send_sem.at[k - 1],
            recv_sem=recv_sem.at[k - 1],
            device_id={axis: peer},
            device_id_type=MESH,
        )
        copy.start()
        copies.append(copy)
    return copies


def gather(axis, n, ref, send_sem, recv_sem):
    me = lax.axis_index(axis)
    return post(axis, n, lambda peer: ref.at[me], lambda k: ref.at[me], send_sem, recv_sem)


def scatter(axis, n, out, into, send_sem, recv_sem):
    return post(axis, n, lambda peer: out.at[peer], lambda k: into.at[k], send_sem, recv_sem)


def finish(*groups):
    for copies in groups:
        for copy in copies:
            copy.wait()


def total(own, into, n):
    acc = own.astype(F32)
    for k in range(n - 1):
        acc = acc + into[k].astype(F32)
    return acc


def attend(keys, values, q, c):
    scale = HEAD ** (-0.5)
    scores = lax.dot_general(keys, q, COLS, preferred_element_type=F32) * scale
    weights = jnp.exp(scores - jnp.max(scores, axis=0, keepdims=True))
    probs = weights / jnp.sum(weights, axis=0, keepdims=True)
    probs_bf = probs.astype(BF16)
    dprob = lax.dot_general(values, c, COLS, preferred_element_type=F32)
    delta = jnp.sum(probs_bf.astype(F32) * dprob, axis=0, keepdims=True)
    dscore = (probs * (dprob - delta) * scale).astype(BF16)
    query_grad = lax.dot_general(dscore, keys, ROWS, preferred_element_type=F32).astype(BF16)
    key_grad = jnp.dot(dscore, q, preferred_element_type=F32).astype(BF16)
    value_grad = jnp.dot(probs_bf, c, preferred_element_type=F32).astype(BF16)
    return query_grad, key_grad, value_grad


def step_kernel(
    S, N, x_ref, mg_ref, fg_ref, wg_hbm, wu_hbm, wd_hbm, wk_hbm, wv_hbm, q_hbm, c_hbm,
    qg_hbm, hg_out, normed_out, hid_out, oall_out, gate_out, up_out,
    wg, wu, wd, wk, wv, q, c, qg,
    xg, sqs, sqr, gus, gur, hid_all, inv_all, ds, dr, feat, sqo, enc, af, eg,
    r6, s6, r6b, pin, oall, s9, r9, aall, s11, r11, pin2,
    load_sem, store_sem, ssem, rsem,
):
    tt, F = x_ref.shape
    T = N * tt
    ts = T // S
    H = wg.shape[1]
    D = F * S
    heads = q.shape[1] // HEAD
    sec = lax.axis_index("section")
    ten = lax.axis_index("tensor")
    loads = [
        pltpu.make_async_copy(src, dst, load_sem.at[i])
        for i, (src, dst) in enumerate((
            (wg_hbm, wg), (wu_hbm, wu), (wd_hbm, wd), (wk_hbm, wk), (wv_hbm, wv),
            (q_hbm, q), (c_hbm, c),
        ))
    ]
    for load in loads[:3]:
        load.start()
    xg[ten] = x_ref[...]
    enter((("section", S), ("tensor", N)))
    finish(post("tensor", N, lambda p: x_ref, lambda k: xg.at[ten], ssem.at[0], rsem.at[0]))
    wide = xg[...].reshape(T, F).astype(F32)
    scaled = (wide * mg_ref[...]).astype(BF16)
    square = jnp.sum(wide * wide, axis=1, keepdims=True)
    sqs[...] = jnp.broadcast_to(square, (T, LANES)).reshape(S, ts, LANES)
    loads[0].wait()
    gus[0] = jnp.dot(scaled, wg[...], preferred_element_type=F32).astype(BF16).reshape(S, ts, H)
    move_q = scatter("section", S, sqs, sqr, ssem.at[3], rsem.at[3])
    move_g = scatter("section", S, gus.at[0], gur.at[0], ssem.at[1], rsem.at[1])
    loads[1].wait()
    gus[1] = jnp.dot(scaled, wu[...], preferred_element_type=F32).astype(BF16).reshape(S, ts, H)
    move_u = scatter("section", S, gus.at[1], gur.at[1], ssem.at[2], rsem.at[2])
    for load in loads[3:]:
        load.start()
    finish(move_q, move_g)
    inv = lax.rsqrt(total(sqs[sec], sqr, S) / D + EPSILON)
    inv_all[sec] = inv
    inv = inv[:, :1]
    gate_pre = total(gus[0, sec], gur.at[0], S) * inv
    sig = jax.nn.sigmoid(gate_pre)
    act = gate_pre * sig
    af[0, sec] = act.astype(BF16)
    slope = sig * (1.0 + gate_pre * (1.0 - sig))
    finish(move_u)
    up_pre = total(gus[1, sec], gur.at[1], S) * inv
    hid_all[sec] = (act * up_pre).astype(BF16)
    move_h = gather("section", S, hid_all, ssem.at[4], rsem.at[4])
    move_i = gather("section", S, inv_all, ssem.at[5], rsem.at[5])
    af[1, sec] = (up_pre * slope).astype(BF16)
    loads[2].wait()
    finish(move_h)
    hid = hid_all[...].reshape(T, H)
    ds[...] = jnp.dot(hid, wd[...], preferred_element_type=F32).astype(BF16).reshape(N, tt, F)
    move_d = scatter("tensor", N, ds, dr, ssem.at[6], rsem.at[6])
    hid_out[...] = hid
    finish(move_i)
    inv_tok = inv_all[...].reshape(T, LANES)
    normed_out[...] = (wide * inv_tok[:, :1] * mg_ref[...]).astype(BF16)
    finish(move_d)
    outer = x_ref[...].astype(F32) + total(ds[ten], dr, N)
    feat[sec] = (outer * fg_ref[...]).astype(BF16)
    sqo[sec] = jnp.broadcast_to(jnp.sum(outer * outer, axis=1, keepdims=True), (tt, LANES))
    move_s = gather("section", S, sqo, ssem.at[8], rsem.at[8])
    move_f = gather("section", S, feat, ssem.at[7], rsem.at[7])
    finish(move_s, move_f)
    move_act = gather("section", S, af.at[0], ssem.at[10], rsem.at[10])
    move_fac = gather("section", S, af.at[1], ssem.at[11], rsem.at[11])
    inv_o = lax.rsqrt(jnp.sum(sqo[...], axis=0) / D + EPSILON)
    enc[ten] = (feat[...].astype(F32) * inv_o[None, :, :1]).astype(BF16)
    inv_o = inv_o[:, :1]
    move_e = gather("tensor", N, enc, ssem.at[9], rsem.at[9])
    for load in loads[3:]:
        load.wait()
    finish(move_e)

    width = heads * HEAD
    keys = jnp.zeros((T, width), F32)
    values = jnp.zeros((T, width), F32)
    for s in range(S):
        block = enc[:, s].reshape(T, F)
        keys += jnp.dot(block, wk[s * F : (s + 1) * F, :], preferred_element_type=F32)
        values += jnp.dot(block, wv[s * F : (s + 1) * F, :], preferred_element_type=F32)
    keys = keys.astype(BF16)
    values = values.astype(BF16)
    key_grads, value_grads, stores = [], [], []
    for h in range(heads):
        cols = slice(h * HEAD, (h + 1) * HEAD)
        query_grad, key_grad, value_grad = attend(
            keys[:, cols], values[:, cols], q[:, cols], c[:, cols]
        )
        qg[h] = query_grad
        store = pltpu.make_async_copy(qg.at[h], qg_hbm.at[:, cols], store_sem.at[h])
        store.start()
        stores.append(store)
        key_grads.append(key_grad)
        value_grads.append(value_grad)
    key_grad = jnp.concatenate(key_grads, axis=1)
    value_grad = jnp.concatenate(value_grads, axis=1)
    for s in range(S):
        rows = slice(s * F, (s + 1) * F)
        part = lax.dot_general(key_grad, wk[rows, :], COLS, preferred_element_type=F32)
        part += lax.dot_general(value_grad, wv[rows, :], COLS, preferred_element_type=F32)
        eg[:, s] = part.astype(BF16).reshape(N, tt, F)

    finish(scatter("tensor", N, eg, r6, ssem.at[12], rsem.at[12]))
    s6[...] = total(eg[ten], r6, N).astype(BF16)
    finish(scatter("section", S, s6, r6b, ssem.at[13], rsem.at[13]))
    scaled_out = fg_ref[...] * total(s6[sec], r6b, S)
    pin[sec] = jnp.broadcast_to(
        jnp.sum(scaled_out * outer, axis=1, keepdims=True), (tt, LANES)
    )
    finish(gather("section", S, pin, ssem.at[14], rsem.at[14]))
    inner = jnp.sum(pin[...], axis=0)[:, :1] / D
    outer_grad = inv_o * scaled_out - outer * (inv_o * inv_o * inv_o * inner)
    oall[ten] = outer_grad.astype(BF16)
    finish(gather("tensor", N, oall, ssem.at[15], rsem.at[15]))
    grads = oall[...].reshape(T, F)
    half = H // 2
    moves = []
    for i in range(2):
        s9[i] = (
            lax.dot_general(
                grads, wd[i * half : (i + 1) * half, :], COLS, preferred_element_type=F32
            )
            .astype(BF16)
            .reshape(S, ts, half)
        )
        moves.append(scatter("section", S, s9.at[i], r9.at[i], ssem.at[16 + i], rsem.at[16 + i]))
    oall_out[...] = grads
    finish(move_act, move_fac)
    gathers = []
    for i in range(2):
        finish(moves[i])
        aall[i, sec] = total(s9[i, sec], r9.at[i], S).astype(BF16)
        gathers.append(gather("section", S, aall.at[i], ssem.at[18 + i], rsem.at[18 + i]))
    parts = None
    for i in range(2):
        cols = slice(i * half, (i + 1) * half)
        finish(gathers[i])
        act_grad = aall[i].reshape(T, half).astype(F32)
        up_grad = (act_grad * af[0, :, :, cols].reshape(T, half).astype(F32)).astype(BF16)
        gate_grad = (act_grad * af[1, :, :, cols].reshape(T, half).astype(F32)).astype(BF16)
        up_out[:, cols] = up_grad
        gate_out[:, cols] = gate_grad
        part = lax.dot_general(gate_grad, wg[:, cols], COLS, preferred_element_type=F32)
        part += lax.dot_general(up_grad, wu[:, cols], COLS, preferred_element_type=F32)
        parts = part if parts is None else parts + part
    s11[...] = parts.astype(BF16).reshape(N, tt, F)
    finish(scatter("tensor", N, s11, r11, ssem.at[20], rsem.at[20]))
    hidden = x_ref[...].astype(F32)
    scaled_in = mg_ref[...] * total(s11[ten], r11, N)
    pin2[sec] = jnp.broadcast_to(
        jnp.sum(scaled_in * hidden, axis=1, keepdims=True), (tt, LANES)
    )
    finish(gather("section", S, pin2, ssem.at[21], rsem.at[21]))
    inner_in = jnp.sum(pin2[...], axis=0)[:, :1] / D
    inv_flat = inv_all.reshape(T, LANES)
    inv_in = inv_flat[pl.ds(pl.multiple_of(ten * tt, tt), tt), :][:, :1]
    hg_out[...] = (
        outer_grad + inv_in * scaled_in - hidden * (inv_in * inv_in * inv_in * inner_in)
    )
    for store in stores:
        store.wait()


def on_device(
    S, N, enc_hidden, mlp_gain, final_gain, w_gate, w_up, w_down, key_weight, value_weight,
    queries, context_grad,
):
    tt, F = enc_hidden.shape
    T = N * tt
    ts = T // S
    H = w_gate.shape[1]
    peers = max(S, N) - 1
    vmem = pl.BlockSpec(memory_space=pltpu.VMEM)
    hbm = pl.BlockSpec(memory_space=pl.ANY)
    shape = jax.ShapeDtypeStruct
    dma = pltpu.SemaphoreType.DMA
    wk, wv, q, c = key_weight[0], value_weight[0], queries[0], context_grad[0]
    large = (w_gate, w_up, w_down, wk, wv, q, c)
    rows = q.shape[0]
    heads = q.shape[1] // HEAD
    scratch = [pltpu.VMEM(w.shape, BF16) for w in large]
    scratch += [
        pltpu.VMEM((heads, rows, HEAD), BF16),
        pltpu.VMEM((N, tt, F), BF16),
        pltpu.VMEM((S, ts, LANES), F32),
        pltpu.VMEM((S - 1, ts, LANES), F32),
        pltpu.VMEM((2, S, ts, H), BF16),
        pltpu.VMEM((2, S - 1, ts, H), BF16),
        pltpu.VMEM((S, ts, H), BF16),
        pltpu.VMEM((S, ts, LANES), F32),
        pltpu.VMEM((N, tt, F), BF16),
        pltpu.VMEM((N - 1, tt, F), BF16),
        pltpu.VMEM((S, tt, F), BF16),
        pltpu.VMEM((S, tt, LANES), F32),
        pltpu.VMEM((N, S, tt, F), BF16),
        pltpu.VMEM((2, S, ts, H), BF16),
        pltpu.VMEM((N, S, tt, F), BF16),
        pltpu.VMEM((N - 1, S, tt, F), BF16),
        pltpu.VMEM((S, tt, F), BF16),
        pltpu.VMEM((S - 1, tt, F), BF16),
        pltpu.VMEM((S, tt, LANES), F32),
        pltpu.VMEM((N, tt, F), BF16),
        pltpu.VMEM((2, S, ts, H // 2), BF16),
        pltpu.VMEM((2, S - 1, ts, H // 2), BF16),
        pltpu.VMEM((2, S, ts, H // 2), BF16),
        pltpu.VMEM((N, tt, F), BF16),
        pltpu.VMEM((N - 1, tt, F), BF16),
        pltpu.VMEM((S, tt, LANES), F32),
        dma((7,)), dma((heads,)), dma((22, peers)), dma((22, peers)),
    ]
    query_grad, hidden_grad, normed, hid, outer_all, gate_all, up_all = pl.pallas_call(
        functools.partial(step_kernel, S, N),
        out_shape=[
            shape(q.shape, BF16), shape((tt, F), F32), shape((T, F), BF16),
            shape((T, H), BF16), shape((T, F), BF16), shape((T, H), BF16), shape((T, H), BF16),
        ],
        in_specs=[vmem] * 3 + [hbm] * 7,
        out_specs=[hbm] + [vmem] * 6,
        scratch_shapes=scratch,
        compiler_params=pltpu.CompilerParams(
            collective_id=0, has_side_effects=True, vmem_limit_bytes=VMEM_LIMIT
        ),
    )(enc_hidden, mlp_gain[None, :], final_gain[None, :], *large)

    outer_product = lambda a, b: lax.dot_general(
        a, b, ROWS, preferred_element_type=F32
    ).astype(BF16)
    return (
        query_grad[None, :, :],
        hidden_grad,
        outer_product(normed, gate_all),
        outer_product(normed, up_all),
        outer_product(hid, outer_all),
    )


def solution(mesh):
    in_specs = (
        P(("dp", "tensor"), "section"),
        P("section"),
        P("section"),
        P("section", "tensor"),
        P("section", "tensor"),
        P("tensor", "section"),
        P("section", None, "tensor"),
        P("section", None, "tensor"),
        P("section", "dp", "tensor"),
        P("section", "dp", "tensor"),
    )
    out_specs = (
        P("section", "dp", "tensor"),
        P(("dp", "tensor"), "section"),
        P(("dp", "section"), "tensor"),
        P(("dp", "section"), "tensor"),
        P(("dp", "tensor"), "section"),
    )
    body = functools.partial(on_device, mesh.shape["section"], mesh.shape["tensor"])
    return jax.shard_map(
        body, mesh=mesh, in_specs=in_specs, out_specs=out_specs, check_vma=False
    )
```

time: 116 us -> 94.9 us (0.82)
  Pallas kernels: 97.5 us -> 84.8 us
  local copies, waits for them, and re-layouts: 11.3 us -> 1.96 us
    pallas_call x3 -> x1, Pallas kernels: 97.5 us -> 84.8 us  [on_device(): pl.pallas_call(functools.partial(step_kernel, S, N), out_shape=[shape(q.s...]
    unnamed x27 -> x14, local copies, waits for them, and re-layouts: 11.3 us -> 1.96 us
where the time goes in v2:
time: 94.9 us; the launch traced here: 94.6 us
  Pallas kernels  84.8 us (89%)
  matrix products  7.19 us (8%)
  local copies, waits for them, and re-layouts  1.96 us (2%)
    pallas_call x1, Pallas kernels, on_device(): pl.pallas_call(functools.partial(step_kernel, S, N), out_shape=[shape(q.s...  84.8 us
    dot_general x3, matrix products, on_device(): lax.dot_general(a, b, ROWS, preferred_element_type=F32).astype(BF16)  7.19 us
    unnamed x14, local copies, waits for them, and re-layouts  1.96 us

profile of v2, /device:TPU:0, one launch (start us, length us, event | category | flops | bytes accessed | tf_op | source)
XLA Modules:
  0.0 94.6 jit_solution(2543089153661333619)
XLA Ops:
  0.6 84.8 %shard_map.137 = (bf16[1024,1024]{1,0:T(8,128)(2,1)}, f32[16,512]{1,0:T(8,128)}, bf16[64,512]{1,0:T(8,128)(2,1)}, bf16[64,2048]{1,0:T(8,128)(2,1)}, bf16[64,512]...) custom-call(bf16[16,512]{1,0:T(8,128)(2,1)} %x_ref.1, f32[1,512]{1,0:T(1,128)} %bitcast.18, ...), custom_call_target="tpu_custom_call" | custom-call | tf_op jit(solution)/shard_map/pallas_call | solution.py:305
  85.4 0.0 copy-start.2
  85.4 0.0 copy-start.3
  85.5 0.0 copy-start.1
  85.5 0.0 copy-start.4
  85.5 3.1 %convolution_convert_fusion.2 = bf16[512,2048]{1,0:T(8,128)(2,1)} fusion(bf16[64,512]{1,0:T(8,128)(2,1)} %get-tuple-element.14, bf16[64,2048]{1,0:T(8,128)(2,1)} %get-tuple-element.15), kind=kOutput, calls=%fused_computation.2 | convolution fusion | flops 135266304 | bytes 2424832 | tf_op jit(solution)/shard_map/dot_general | solution.py:319
  88.6 0.0 copy-done.2
  88.6 0.0 copy-done.3
  88.6 0.0 copy-start
  88.6 2.0 %convolution_convert_fusion.1 = bf16[512,2048]{1,0:T(8,128)(2,1)} fusion(bf16[64,512]{1,0:T(8,128)(2,1)S(1)} %copy-done.3, bf16[64,2048]{1,0:T(8,128)(2,1)S(1)} %copy-done.2), kind=kOutput, calls=%fused_computation.1 | convolution fusion | flops 135266304 | bytes 2424832 | tf_op jit(solution)/shard_map/dot_general | solution.py:319
  90.6 0.0 copy-done.1
  90.6 0.0 copy-done.4
  90.6 2.1 %convolution_convert_fusion = bf16[2048,512]{1,0:T(8,128)(2,1)} fusion(bf16[64,2048]{1,0:T(8,128)(2,1)S(1)} %copy-done.1, bf16[64,512]{1,0:T(8,128)(2,1)S(1)} %copy-done.4), kind=kOutput, calls=%fused_computation | convolution fusion | flops 135266304 | bytes 2424832 | tf_op jit(solution)/shard_map/dot_general | solution.py:319
  92.7 0.0 copy-done
  92.7 0.0 copy-start.5
  92.7 1.3 %copy.17 = bf16[1,1024,1024]{2,1,0:T(8,128)(2,1)} copy(bf16[1,1024,1024]{2,1,0:T(8,128)(2,1)S(1)} %bitcast.17) | data formatting | bytes 4194304
  94.0 0.0 copy-done.5
  94.0 0.6 copy.18
Async XLA Ops:
  85.4 3.1 %copy-start.2 = (bf16[64,2048]{1,0:T(8,128)(2,1)S(1)}, bf16[64,2048]{1,0:T(8,128)(2,1)}, u32[]{:S(2)}) copy-start(bf16[64,2048]{1,0:T(8,128)(2,1)} %get-tuple-element.16) | copy-start | bytes 786436
  85.4 3.1 %copy-start.3 = (bf16[64,512]{1,0:T(8,128)(2,1)S(1)}, bf16[64,512]{1,0:T(8,128)(2,1)}, u32[]{:S(2)}) copy-start(bf16[64,512]{1,0:T(8,128)(2,1)} %get-tuple-element.14) | copy-start | bytes 196612
  85.5 5.2 %copy-start.1 = (bf16[64,2048]{1,0:T(8,128)(2,1)S(1)}, bf16[64,2048]{1,0:T(8,128)(2,1)}, u32[]{:S(2)}) copy-start(bf16[64,2048]{1,0:T(8,128)(2,1)} %get-tuple-element.17) | copy-start | bytes 786436
  85.5 5.2 %copy-start.4 = (bf16[64,512]{1,0:T(8,128)(2,1)S(1)}, bf16[64,512]{1,0:T(8,128)(2,1)}, u32[]{:S(2)}) copy-start(bf16[64,512]{1,0:T(8,128)(2,1)} %get-tuple-element.18) | copy-start | bytes 196612
  88.6 4.1 %copy-start = (bf16[1024,1024]{1,0:T(8,128)(2,1)S(1)}, bf16[1024,1024]{1,0:T(8,128)(2,1)}, u32[]{:S(2)}) copy-start(bf16[1024,1024]{1,0:T(8,128)(2,1)} %get-tuple-element.12) | copy-start | bytes 6291460
  92.7 1.3 %copy-start.5 = (f32[16,512]{1,0:T(8,128)S(1)}, f32[16,512]{1,0:T(8,128)}, u32[]{:S(2)}) copy-start(f32[16,512]{1,0:T(8,128)} %get-tuple-element.25) | copy-start | bytes 98308
